TPU v7x, 32 devices: a whole 2x2x4 slice. The times are simulated.
32 devices in a mesh: dp: 8 (over z, x), tensor: 4 (over y, core).
Axes of the slice: x: 2, y: 2, z: 4, core: 2. Of those that a mesh axis runs over, the one named last changes fastest.
Arguments:
- lang_in: bfloat16 [3840, 768], P(('dp', 'tensor')), may hold values from -6 to 6
- visn_in: bfloat16 [6912, 768], P(('dp', 'tensor')), may hold values from -6 to 6
- word_mask: int32 [192, 20], P('dp'), may hold values from 0 to 1, as said below
- task_flag: int32 [192], P('dp'), may hold values from 0 to 2
- group_id: int32 [192], P('dp'), may hold values from 0 to 4
- task_table: bfloat16 [3, 768], replicated, may hold values from -3 to 3
- group_table: bfloat16 [5, 768], replicated, may hold values from -3 to 3
- attn_in: bfloat16 [3, 3, 768, 768], P(None, None, None, 'tensor'), may hold values from -0.21875 to 0.21875
- attn_qv_bias: bfloat16 [3, 2, 768], P(None, None, 'tensor'), may hold values from -3 to 3
- attn_out: bfloat16 [3, 768, 768], P(None, 'tensor'), may hold values from -0.625 to 0.625
- ffn_in: bfloat16 [2, 768, 3072], P(None, None, 'tensor'), may hold values from -0.21875 to 0.21875
- ffn_in_bias: bfloat16 [2, 3072], P(None, 'tensor'), may hold values from -3 to 3
- ffn_out: bfloat16 [2, 3072, 768], P(None, 'tensor'), may hold values from -0.15625 to 0.15625
- out_bias: bfloat16 [5, 768], replicated, may hold values from -2 to 2
- norm_gain: bfloat16 [5, 768], replicated, may hold values from 0.099609375 to 1.8984375
- norm_bias: bfloat16 [5, 768], replicated, may hold values from -2 to 2
- lang_cot: bfloat16 [3840, 768], P(('dp', 'tensor')), may hold values from -6 to 6
- visn_cot: bfloat16 [6912, 768], P(('dp', 'tensor')), may hold values from -6 to 6
Outputs:
- lang_out: bfloat16 [3840, 768], P(('dp', 'tensor'))
- visn_out: bfloat16 [6912, 768], P(('dp', 'tensor'))
- lang_grad: bfloat16 [3840, 768], P(('dp', 'tensor'))
- visn_grad: bfloat16 [6912, 768], P(('dp', 'tensor'))
- task_grad: float32 [3, 768], replicated
- group_grad: float32 [5, 768], replicated
- attn_in_grad: float32 [3, 3, 768, 768], P(None, None, 'dp', 'tensor')
- qv_bias_grad: float32 [3, 2, 768], P(None, None, 'tensor')
- attn_out_grad: float32 [3, 768, 768], P(None, 'tensor', 'dp')
- ffn_in_grad: float32 [2, 768, 3072], P(None, 'dp', 'tensor')
- ffn_bias_grad: float32 [2, 3072], P(None, 'tensor')
- ffn_out_grad: float32 [2, 3072, 768], P(None, 'tensor', 'dp')
- out_bias_grad: float32 [5, 768], replicated
- gain_grad: float32 [5, 768], replicated
- shift_grad: float32 [5, 768], replicated
Inputs may be any that keep to these rules, and one draw needn't show every extreme that they name: `word_mask`: each item's mask is 1 on its first 6 to 20 word slots and 0 after them.
All inputs are finite; a program needn't handle non-finite values.
Results may differ from a plain program's by a relative error of at most 0.035.
Values may be sent and summed in bfloat16 or wider, within the bound.
A program may use at most 192 MiB of HBM per device.

v0:
```python
import jax
import jax.numpy as jnp
from jax import lax
from jax.sharding import PartitionSpec as P

HEAD = 64
WORDS = 20
REGIONS = 36
TASKS = 3
GROUPS = 5


norm_eps = 1e-06
root_half = 0.7071067811865476
inv_root_tau = 0.3989422804014327
highest = lax.Precision.HIGHEST


def linear(source, weight):
    return jnp.dot(source, weight, preferred_element_type=jnp.float32)


def linear_back(upstream, weight):
    return lax.dot_general(
        upstream, weight, (((1,), (1,)), ((), ())), preferred_element_type=jnp.float32
    )


def weight_grad(source, upstream):
    return lax.dot_general(
        source, upstream, (((0,), (0,)), ((), ())), preferred_element_type=jnp.float32
    )


def column_sum(upstream):
    return jnp.sum(upstream.astype(jnp.float32), axis=0)


def gelu_value(pre_act):
    return 0.5 * pre_act * (1.0 + lax.erf(pre_act * root_half))


def gelu_slope(pre_act):
    return (
        0.5 * (1.0 + lax.erf(pre_act * root_half))
        + pre_act * jnp.exp(-0.5 * pre_act * pre_act) * inv_root_tau
    )


def norm_forward(pre_norm, gain_vec, shift_vec):
    average = jnp.mean(pre_norm, axis=-1, keepdims=True)
    centred = pre_norm - average
    spread = jnp.mean(centred * centred, axis=-1, keepdims=True)
    inverse = lax.rsqrt(spread + norm_eps)
    normed = centred * inverse
    return (normed * gain_vec + shift_vec, (normed, inverse))


def norm_backward(out_grad, stash, gain_vec):
    normed, inverse = stash
    scaled = out_grad * gain_vec
    in_grad = inverse * (
        scaled
        - jnp.mean(scaled, axis=-1, keepdims=True)
        - normed * jnp.mean(scaled * normed, axis=-1, keepdims=True)
    )
    return (
        in_grad,
        jnp.sum(out_grad * normed, axis=0),
        jnp.sum(out_grad, axis=0),
        jnp.sum(in_grad, axis=0),
    )


def split_heads(flattened, item_count):
    return flattened.reshape(
        item_count, flattened.shape[0] // item_count, flattened.shape[1] // HEAD, HEAD
    )


def merge_heads(split_rows):
    return split_rows.reshape(
        split_rows.shape[0] * split_rows.shape[1], split_rows.shape[2] * split_rows.shape[3]
    )


def attend_forward(source_q, source_kv, keep_mask, weights, biases, item_count):
    queries = (linear(source_q, weights[0]) + biases[0]).astype(jnp.bfloat16)
    key_rows = linear(source_kv, weights[1]).astype(jnp.bfloat16)
    values = (linear(source_kv, weights[2]) + biases[1]).astype(jnp.bfloat16)
    score_scale = HEAD ** (-0.5)
    scores = (
        jnp.einsum(
            "bqhd,bkhd->bhqk",
            split_heads(queries, item_count),
            split_heads(key_rows, item_count),
            preferred_element_type=jnp.float32,
        )
        * score_scale
    )
    if keep_mask is not None:
        scores = jnp.where(keep_mask[:, None, None, :], scores, -1000000000.0)
    row_max = jnp.max(scores, axis=-1, keepdims=True)
    powers = jnp.exp(scores - row_max)
    attn_probs = powers / jnp.sum(powers, axis=-1, keepdims=True)
    probs_low = attn_probs.astype(jnp.bfloat16)
    context = jnp.einsum(
        "bhqk,bkhd->bqhd",
        probs_low,
        split_heads(values, item_count),
        preferred_element_type=jnp.float32,
    )
    context = merge_heads(context).astype(jnp.bfloat16)
    return (context, (queries, key_rows, values, attn_probs, probs_low))


def attend_backward(grad_context, stash, item_count):
    queries, key_rows, values, attn_probs, probs_low = stash
    score_scale = HEAD ** (-0.5)
    grad_heads = split_heads(grad_context.astype(jnp.bfloat16), item_count)
    grad_probs = jnp.einsum(
        "bqhd,bkhd->bhqk",
        grad_heads,
        split_heads(values, item_count),
        preferred_element_type=jnp.float32,
    )
    grad_values = jnp.einsum(
        "bhqk,bqhd->bkhd", probs_low, grad_heads, preferred_element_type=jnp.float32
    )
    grad_scores = attn_probs * (
        grad_probs - jnp.sum(grad_probs * attn_probs, axis=-1, keepdims=True)
    )
    scores_low = grad_scores.astype(jnp.bfloat16)
    grad_query = (
        jnp.einsum(
            "bhqk,bkhd->bqhd",
            scores_low,
            split_heads(key_rows, item_count),
            preferred_element_type=jnp.float32,
        )
        * score_scale
    )
    grad_keys = (
        jnp.einsum(
            "bhqk,bqhd->bkhd",
            scores_low,
            split_heads(queries, item_count),
            preferred_element_type=jnp.float32,
        )
        * score_scale
    )
    return (
        merge_heads(grad_query).astype(jnp.bfloat16),
        merge_heads(grad_keys).astype(jnp.bfloat16),
        merge_heads(grad_values).astype(jnp.bfloat16),
    )


def projection_grads(source_q, source_kv, weights, grad_set):
    grad_query, grad_keys, grad_values = grad_set
    w_grads = jnp.stack(
        [
            weight_grad(source_q, grad_query),
            weight_grad(source_kv, grad_keys),
            weight_grad(source_kv, grad_values),
        ]
    )
    b_grads = jnp.stack([column_sum(grad_query), column_sum(grad_values)])
    back_query = linear_back(grad_query, weights[0])
    back_kv = linear_back(grad_keys, weights[1]) + linear_back(grad_values, weights[2])
    return (w_grads, b_grads, back_query, back_kv)


def gather_rows(former, latter):
    return (
        lax.all_gather(former, "tensor", axis=0, tiled=True),
        lax.all_gather(latter, "tensor", axis=0, tiled=True),
    )


def scatter_rows(former, latter):
    return (
        lax.psum_scatter(
            former.astype(jnp.bfloat16), "tensor", scatter_dimension=0, tiled=True
        ).astype(jnp.float32),
        lax.psum_scatter(
            latter.astype(jnp.bfloat16), "tensor", scatter_dimension=0, tiled=True
        ).astype(jnp.float32),
    )


def gather_grads(former, latter):
    return (
        lax.all_gather(former, "tensor", axis=0, tiled=True),
        lax.all_gather(latter, "tensor", axis=0, tiled=True),
    )


def scatter_grads(former, latter):
    return (
        lax.psum_scatter(
            former.astype(jnp.bfloat16), "tensor", scatter_dimension=0, tiled=True
        ).astype(jnp.float32),
        lax.psum_scatter(
            latter.astype(jnp.bfloat16), "tensor", scatter_dimension=0, tiled=True
        ).astype(jnp.float32),
    )


def body(
    lang_in,
    visn_in,
    word_mask,
    task_flag,
    group_id,
    task_table,
    group_table,
    attn_in,
    attn_qv_bias,
    attn_out,
    ffn_in,
    ffn_in_bias,
    ffn_out,
    out_bias,
    norm_gain,
    norm_bias,
    lang_cot,
    visn_cot,
):
    item_count = word_mask.shape[0]
    lang_rows = lang_in.shape[0]
    visn_rows = visn_in.shape[0]
    tensor_place = lax.axis_index("tensor")
    item_ids = jnp.arange(item_count, dtype=jnp.int32)
    lang_item = (tensor_place * lang_rows + jnp.arange(lang_rows, dtype=jnp.int32)) // WORDS
    visn_item = (tensor_place * visn_rows + jnp.arange(visn_rows, dtype=jnp.int32)) // REGIONS
    lang_pick = (lang_item[:, None] == item_ids[None, :]).astype(jnp.bfloat16)
    visn_pick = (visn_item[:, None] == item_ids[None, :]).astype(jnp.bfloat16)
    task_pick = (task_flag[:, None] == jnp.arange(TASKS, dtype=jnp.int32)[None, :]).astype(
        jnp.bfloat16
    )
    group_pick = (group_id[:, None] == jnp.arange(GROUPS, dtype=jnp.int32)[None, :]).astype(
        jnp.bfloat16
    )
    lang_task = linear(lang_pick, task_pick)
    visn_group = linear(visn_pick, group_pick)
    lang_base = lang_in.astype(jnp.float32) + linear(lang_task.astype(jnp.bfloat16), task_table)
    visn_base = visn_in.astype(jnp.float32) + linear(visn_group.astype(jnp.bfloat16), group_table)
    gains = norm_gain.astype(jnp.float32)
    shifts = norm_bias.astype(jnp.float32)
    offsets = out_bias.astype(jnp.float32)
    qv_bias = attn_qv_bias.astype(jnp.float32)
    hidden_bias = ffn_in_bias.astype(jnp.float32)
    keep_words = word_mask > 0
    lang_low = lang_base.astype(jnp.bfloat16)
    visn_low = visn_base.astype(jnp.bfloat16)
    lang_all, visn_all = gather_rows(lang_low, visn_low)
    cross_lang = attend_forward(lang_all, visn_all, None, attn_in[0], qv_bias[0], item_count)[0]
    cross_visn = attend_forward(visn_all, lang_all, keep_words, attn_in[0], qv_bias[0], item_count)[
        0
    ]
    part_lang, part_visn = scatter_rows(
        linear(cross_lang, attn_out[0]), linear(cross_visn, attn_out[0])
    )
    lang_one, stash_l0 = norm_forward(lang_base + part_lang + offsets[0], gains[0], shifts[0])
    visn_one, stash_v0 = norm_forward(visn_base + part_visn + offsets[0], gains[0], shifts[0])
    self_lang, self_visn = gather_rows(lang_one.astype(jnp.bfloat16), visn_one.astype(jnp.bfloat16))
    ctx_lang, saved_lang = attend_forward(
        self_lang, self_lang, keep_words, attn_in[1], qv_bias[1], item_count
    )
    ctx_visn, saved_visn = attend_forward(
        self_visn, self_visn, None, attn_in[2], qv_bias[2], item_count
    )
    part_lang, part_visn = scatter_rows(
        linear(ctx_lang, attn_out[1]), linear(ctx_visn, attn_out[2])
    )
    lang_two, stash_l1 = norm_forward(lang_one + part_lang + offsets[1], gains[1], shifts[1])
    visn_two, stash_v2 = norm_forward(visn_one + part_visn + offsets[2], gains[2], shifts[2])
    ffn_lang, ffn_visn = gather_rows(lang_two.astype(jnp.bfloat16), visn_two.astype(jnp.bfloat16))
    pre_lang = linear(ffn_lang, ffn_in[0]) + hidden_bias[0]
    pre_visn = linear(ffn_visn, ffn_in[1]) + hidden_bias[1]
    act_lang = gelu_value(pre_lang).astype(jnp.bfloat16)
    act_visn = gelu_value(pre_visn).astype(jnp.bfloat16)
    part_lang, part_visn = scatter_rows(linear(act_lang, ffn_out[0]), linear(act_visn, ffn_out[1]))
    lang_out, stash_l3 = norm_forward(lang_two + part_lang + offsets[3], gains[3], shifts[3])
    visn_out, stash_v4 = norm_forward(visn_two + part_visn + offsets[4], gains[4], shifts[4])
    top_lang, gain_l3, shift_l3, offset_l3 = norm_backward(
        lang_cot.astype(jnp.float32), stash_l3, gains[3]
    )
    top_visn, gain_v4, shift_v4, offset_v4 = norm_backward(
        visn_cot.astype(jnp.float32), stash_v4, gains[4]
    )
    down_lang, down_visn = gather_grads(
        top_lang.astype(jnp.bfloat16), top_visn.astype(jnp.bfloat16)
    )
    ffn_out_grads = jnp.stack([weight_grad(act_lang, down_lang), weight_grad(act_visn, down_visn)])
    inner_lang = (linear_back(down_lang, ffn_out[0]) * gelu_slope(pre_lang)).astype(jnp.bfloat16)
    inner_visn = (linear_back(down_visn, ffn_out[1]) * gelu_slope(pre_visn)).astype(jnp.bfloat16)
    ffn_in_grads = jnp.stack([weight_grad(ffn_lang, inner_lang), weight_grad(ffn_visn, inner_visn)])
    ffn_bias_grads = jnp.stack([column_sum(inner_lang), column_sum(inner_visn)])
    back_lang, back_visn = scatter_grads(
        linear_back(inner_lang, ffn_in[0]), linear_back(inner_visn, ffn_in[1])
    )
    grad_two_lang = top_lang + back_lang
    grad_two_visn = top_visn + back_visn
    top_lang, gain_l1, shift_l1, offset_l1 = norm_backward(grad_two_lang, stash_l1, gains[1])
    top_visn, gain_v2, shift_v2, offset_v2 = norm_backward(grad_two_visn, stash_v2, gains[2])
    mid_lang, mid_visn = gather_grads(top_lang.astype(jnp.bfloat16), top_visn.astype(jnp.bfloat16))
    out_grad_lang = weight_grad(ctx_lang, mid_lang)
    out_grad_visn = weight_grad(ctx_visn, mid_visn)
    grads_lang = attend_backward(linear_back(mid_lang, attn_out[1]), saved_lang, item_count)
    grads_visn = attend_backward(linear_back(mid_visn, attn_out[2]), saved_visn, item_count)
    win_lang, bias_lang, query_lang, kv_lang = projection_grads(
        self_lang, self_lang, attn_in[1], grads_lang
    )
    win_visn, bias_visn, query_visn, kv_visn = projection_grads(
        self_visn, self_visn, attn_in[2], grads_visn
    )
    back_lang, back_visn = scatter_grads(query_lang + kv_lang, query_visn + kv_visn)
    grad_one_lang = top_lang + back_lang
    grad_one_visn = top_visn + back_visn
    top_lang, gain_l0, shift_l0, offset_l0 = norm_backward(grad_one_lang, stash_l0, gains[0])
    top_visn, gain_v0, shift_v0, offset_v0 = norm_backward(grad_one_visn, stash_v0, gains[0])
    cross_dlang, cross_dvisn = gather_grads(
        top_lang.astype(jnp.bfloat16), top_visn.astype(jnp.bfloat16)
    )
    again_lang, again_visn = (
        lax.all_gather(lang_low, "tensor", axis=0, tiled=True),
        lax.all_gather(visn_low, "tensor", axis=0, tiled=True),
    )
    redo_lang, saved_cross_lang = attend_forward(
        again_lang, again_visn, None, attn_in[0], qv_bias[0], item_count
    )
    redo_visn, saved_cross_visn = attend_forward(
        again_visn, again_lang, keep_words, attn_in[0], qv_bias[0], item_count
    )
    cross_out_grad = weight_grad(redo_lang, cross_dlang) + weight_grad(redo_visn, cross_dvisn)
    grads_cross_lang = attend_backward(
        linear_back(cross_dlang, attn_out[0]), saved_cross_lang, item_count
    )
    grads_cross_visn = attend_backward(
        linear_back(cross_dvisn, attn_out[0]), saved_cross_visn, item_count
    )
    win_first, bias_first, query_from_lang, kv_from_visn = projection_grads(
        again_lang, again_visn, attn_in[0], grads_cross_lang
    )
    win_second, bias_second, query_from_visn, kv_from_lang = projection_grads(
        again_visn, again_lang, attn_in[0], grads_cross_visn
    )
    back_lang, back_visn = scatter_grads(
        query_from_lang + kv_from_lang, query_from_visn + kv_from_visn
    )
    base_grad_lang = top_lang + back_lang
    base_grad_visn = top_visn + back_visn
    attn_in_grads = jnp.stack([win_first + win_second, win_lang, win_visn])
    qv_grads = jnp.stack([bias_first + bias_second, bias_lang, bias_visn])
    attn_out_grads = jnp.stack([cross_out_grad, out_grad_lang, out_grad_visn])
    offset_part = jnp.stack([offset_l0 + offset_v0, offset_l1, offset_v2, offset_l3, offset_v4])
    gain_part = jnp.stack([gain_l0 + gain_v0, gain_l1, gain_v2, gain_l3, gain_v4])
    shift_part = jnp.stack([shift_l0 + shift_v0, shift_l1, shift_v2, shift_l3, shift_v4])
    task_part = lax.dot_general(
        lang_task,
        base_grad_lang,
        (((0,), (0,)), ((), ())),
        precision=highest,
        preferred_element_type=jnp.float32,
    )
    group_part = lax.dot_general(
        visn_group,
        base_grad_visn,
        (((0,), (0,)), ((), ())),
        precision=highest,
        preferred_element_type=jnp.float32,
    )
    attn_in_sum, attn_out_sum, ffn_in_sum, ffn_out_sum, qv_grads, ffn_bias_grads = lax.psum(
        (attn_in_grads, attn_out_grads, ffn_in_grads, ffn_out_grads, qv_grads, ffn_bias_grads), "dp"
    )
    share_rows = attn_in_sum.shape[2] // lax.axis_size("dp")
    share_start = lax.axis_index("dp") * share_rows
    attn_in_grads = lax.dynamic_slice_in_dim(attn_in_sum, share_start, share_rows, 2)
    attn_out_grads = lax.dynamic_slice_in_dim(attn_out_sum, share_start, share_rows, 2)
    ffn_in_grads = lax.dynamic_slice_in_dim(ffn_in_sum, share_start, share_rows, 1)
    ffn_out_grads = lax.dynamic_slice_in_dim(ffn_out_sum, share_start, share_rows, 2)
    task_grad, group_grad, offset_grad, gain_grad, shift_grad = lax.psum(
        (task_part, group_part, offset_part, gain_part, shift_part), ("dp", "tensor")
    )
    return (
        lang_out.astype(jnp.bfloat16),
        visn_out.astype(jnp.bfloat16),
        base_grad_lang.astype(jnp.bfloat16),
        base_grad_visn.astype(jnp.bfloat16),
        task_grad,
        group_grad,
        attn_in_grads,
        qv_grads,
        attn_out_grads,
        ffn_in_grads,
        ffn_bias_grads,
        ffn_out_grads,
        offset_grad,
        gain_grad,
        shift_grad,
    )


def solution(mesh):
    placed = (
        P(("dp", "tensor"), None),
        P(("dp", "tensor"), None),
        P("dp", None),
        P("dp"),
        P("dp"),
        P(),
        P(),
        P(None, None, None, "tensor"),
        P(None, None, "tensor"),
        P(None, "tensor", None),
        P(None, None, "tensor"),
        P(None, "tensor"),
        P(None, "tensor", None),
        P(),
        P(),
        P(),
        P(("dp", "tensor"), None),
        P(("dp", "tensor"), None),
    )
    return jax.shard_map(
        body,
        mesh=mesh,
        in_specs=placed,
        out_specs=(
            P(("dp", "tensor"), None),
            P(("dp", "tensor"), None),
            P(("dp", "tensor"), None),
            P(("dp", "tensor"), None),
            P(),
            P(),
            P(None, None, "dp", "tensor"),
            P(None, None, "tensor"),
            P(None, "tensor", "dp"),
            P(None, "dp", "tensor"),
            P(None, "tensor"),
            P(None, "tensor", "dp"),
            P(),
            P(),
            P(),
        ),
        check_vma=False,
    )
```

profile of v0, /device:TPU:8, one launch (start us, length us, event | category | flops | bytes accessed | tf_op | source)
XLA Modules:
  0.0 1207.2 jit_solution(11375417155302913380)
XLA Ops:
  12.5 8.3 all_gather.39
  25.1 5.0 all-gather.7.cloned.1.call-done
  61.5 4.6 fusion.47
  73.7 22.9 %reduce-scatter.13.cloned.1.call-done = bf16[120,768]{1,0:T(8,128)(2,1)} async-done(((bf16[480,768]{1,0:T(8,128)(2,1)}), bf16[120,768]{1,0:T(8,128)(2,1)}) %reduce-scatter.13.cloned.1.call-update) | async-done | bytes 184336 | tf_op jit(solution)/shard_map/reduce_scatter | solution.py:183
  98.3 18.6 %all-gather.9.cloned.1.call-done = bf16[864,768]{1,0:T(8,128)(2,1)} async-done(((bf16[216,768]{1,0:T(8,128)(2,1)}), bf16[864,768]{1,0:T(8,128)(2,1)}) %all-gather.9.cloned.1.call-update) | async-done | bytes 1327120 | tf_op jit(solution)/shard_map/all_gather | solution.py:177
  151.3 8.7 all_gather.40
  180.0 22.5 %reduce-scatter.15.cloned.1.call-done = bf16[120,768]{1,0:T(8,128)(2,1)} async-done(((bf16[480,768]{1,0:T(8,128)(2,1)}), bf16[120,768]{1,0:T(8,128)(2,1)}) %reduce-scatter.15.cloned.1.call-update) | async-done | bytes 184336 | tf_op jit(solution)/shard_map/reduce_scatter | solution.py:183
  204.2 7.8 all_gather.41
  216.6 6.3 all-gather.11.cloned.1.call-done
  222.9 4.6 multiply_convert_fusion
  231.0 17.4 %reduce-scatter.17.cloned.1.call-done = bf16[120,768]{1,0:T(8,128)(2,1)} async-done(((bf16[480,768]{1,0:T(8,128)(2,1)}), bf16[120,768]{1,0:T(8,128)(2,1)}) %reduce-scatter.17.cloned.1.call-update) | async-done | bytes 184336 | tf_op jit(solution)/shard_map/reduce_scatter | solution.py:183
  250.6 26.9 %reduce-scatter.23.cloned.1.call-done = bf16[216,768]{1,0:T(8,128)(2,1)} async-done(((bf16[864,768]{1,0:T(8,128)(2,1)}), bf16[216,768]{1,0:T(8,128)(2,1)}) %reduce-scatter.23.cloned.1.call-update) | async-done | bytes 331792 | tf_op jit(solution)/shard_map/reduce_scatter | solution.py:186
  285.6 10.5 all_gather.44
  302.0 5.0 convert_reduce_fusion
  316.6 10.7 reduce-scatter.25.cloned.1.call-done
  331.0 7.7 all_gather.45
  344.9 11.3 reduce-scatter.29.cloned.1.call-done
  426.0 8.0 all_gather.46
  451.8 5.9 convert_reduce_fusion.5
  501.6 5.0 pad_maximum_fusion.1
  515.8 5.0 pad_maximum_fusion.2
  541.2 35.1 %all-reduce.1 = (f32[3,2,192]{2,1,0:T(2,128)}, f32[2,768]{1,0:T(2,128)}) all-reduce(f32[3,2,192]{2,1,0:T(2,128)S(1)} %pad_maximum_fusion.4, f32[2,768]{1,0:T(2,128)S(1)} %pad_maximum_fusion.5), channel_id=1, replica_groups=mesh['dp'=8,'tensor'=4] {'dp'}, use_global_device_ids=true, to_apply=%region_59.60 | all-reduce | flops 2688 | bytes 21504 | tf_op jit(solution)/shard_map/psum | solution.py:375
  583.5 474.8 %all-reduce.8.cloned.1.call-done = (f32[3,3,768,192]{2,3,1,0:T(8,128)}, f32[3,192,768]{2,1,0:T(8,128)}, f32[2,768,768]{2,1,0:T(8,128)}, f32[2,768,768]{2,1,0:T(8,128)}) async-done(((f32[3,3,768,192]{2,3,1,0:T(8,128)}, f32[3,192,768]{2,1,0:T(8,128)}, f32[2,768,768]{2,1,0:T(8,128)}, f32[2,768,768]{2,1,0:T(8,128)}), (f32[3,3,768,192]{2,3,1,0:T(8,128)}, f32[3,192,768]{2,1,0:T(8,128)}, f32[2,768,768]{2,1,0:T(8,128)}, ...) | async-done | bytes 16515088 | tf_op jit(solution)/shard_map/psum | solution.py:375
  1068.0 125.5 %all-reduce.6.cloned.1.call-done = (f32[3,768]{1,0:T(4,128)}, f32[5,768]{1,0:T(8,128)}, f32[5,768]{1,0:T(8,128)}, f32[5,768]{1,0:T(8,128)}, f32[5,768]{1,0:T(8,128)}) async-done(((f32[3,768]{1,0:T(4,128)}, f32[5,768]{1,0:T(8,128)}, f32[5,768]{1,0:T(8,128)}, f32[5,768]{1,0:T(8,128)}, f32[5,768]{1,0:T(8,128)}), (f32[3,768]{1,0:T(4,128)}, f32[5,768]{1,0:T(8,128)}, f32[5,768]{1,0:T(8,128)}, f32[5,768]{1,0:T(8,128)}, ...) | async-done | bytes 70672 | tf_op jit(solution)/shard_map/psum | solution.py:384
  (659 shorter events, 332.3 us)
Async XLA Ops:
  7.2 22.9 %all-gather.7.cloned.1.call-start = ((), (), s32[]{:S(2)}) async-start(), calls=%async_computation.12 | async-start | bytes 1658880 | tf_op jit(solution)/shard_map/all_gather | solution.py:177
  10.5 60.5 %reduce-scatter.19.cloned.1.call-start = ((), (), s32[]{:S(2)}) async-start(), calls=%async_computation.16 | async-start | bytes 1658880 | tf_op jit(solution)/shard_map/reduce_scatter | solution.py:186
  44.4 52.2 %reduce-scatter.13.cloned.1.call-start = ((), (), s32[]{:S(2)}) async-start(), calls=%async_computation.13 | async-start | bytes 921600 | tf_op jit(solution)/shard_map/reduce_scatter | solution.py:183
  69.0 47.9 %all-gather.9.cloned.1.call-start = ((), (), s32[]{:S(2)}) async-start(), calls=%async_computation.17 | async-start | bytes 1658880 | tf_op jit(solution)/shard_map/all_gather | solution.py:177
  72.3 44.6 %copy-start.106 = (f32[216]{0:T(256)}, f32[216]{0:T(256)S(1)}, u32[]{:S(2)}) copy-start(f32[216]{0:T(256)S(1)} %broadcast_multiply_fusion.8) | copy-start | bytes 2596
  72.5 44.4 %copy-start.111 = (f32[216]{0:T(256)}, f32[216]{0:T(256)S(1)}, u32[]{:S(2)}) copy-start(f32[216]{0:T(256)S(1)} %add_rsqrt_fusion.2) | copy-start | bytes 2596
  73.4 103.8 %reduce-scatter.21.cloned.1.call-start = ((), (), s32[]{:S(2)}) async-start(), calls=%async_computation.18 | async-start | bytes 1658880 | tf_op jit(solution)/shard_map/reduce_scatter | solution.py:186
  150.4 52.0 %reduce-scatter.15.cloned.1.call-start = ((), (), s32[]{:S(2)}) async-start(), calls=%async_computation.14 | async-start | bytes 921600 | tf_op jit(solution)/shard_map/reduce_scatter | solution.py:183
  177.2 45.7 %all-gather.11.cloned.1.call-start = ((), (), s32[]{:S(2)}) async-start(), calls=%async_computation.19 | async-start | bytes 1658880 | tf_op jit(solution)/shard_map/all_gather | solution.py:177
  179.9 68.5 %reduce-scatter.17.cloned.1.call-start = ((), (), s32[]{:S(2)}) async-start(), calls=%async_computation.15 | async-start | bytes 921600 | tf_op jit(solution)/shard_map/reduce_scatter | solution.py:183
  216.5 61.0 %reduce-scatter.23.cloned.1.call-start = ((), (), s32[]{:S(2)}) async-start(), calls=%async_computation.20 | async-start | bytes 1658880 | tf_op jit(solution)/shard_map/reduce_scatter | solution.py:186
  230.9 46.6 %copy-start.116 = (f32[768]{0:T(1024)S(1)}, f32[768]{0:T(1024)}, u32[]{:S(2)}) copy-start(f32[768]{0:T(1024)} %get-tuple-element.83) | copy-start | bytes 9220
  230.9 71.1 %all-gather.13.cloned.1.call-start = ((), (), s32[]{:S(2)}) async-start(), calls=%async_computation.23 | async-start | bytes 1658880 | tf_op jit(solution)/shard_map/all_gather | solution.py:195
  281.4 45.8 %reduce-scatter.25.cloned.1.call-start = ((), (), s32[]{:S(2)}) async-start(), calls=%async_computation.21 | async-start | bytes 921600 | tf_op jit(solution)/shard_map/reduce_scatter | solution.py:201
  301.9 54.3 %reduce-scatter.29.cloned.1.call-start = ((), (), s32[]{:S(2)}) async-start(), calls=%async_computation.24 | async-start | bytes 1658880 | tf_op jit(solution)/shard_map/reduce_scatter | solution.py:204
  310.5 71.5 %all-gather.15.cloned.1.call-start = ((), (), s32[]{:S(2)}) async-start(), calls=%async_computation.25 | async-start | bytes 1658880 | tf_op jit(solution)/shard_map/all_gather | solution.py:195
  359.7 62.6 %reduce-scatter.27.cloned.1.call-start = ((), (), s32[]{:S(2)}) async-start(), calls=%async_computation.22 | async-start | bytes 921600 | tf_op jit(solution)/shard_map/reduce_scatter | solution.py:201
  381.5 62.6 %reduce-scatter.31.cloned.1.call-start = ((), (), s32[]{:S(2)}) async-start(), calls=%async_computation.26 | async-start | bytes 1658880 | tf_op jit(solution)/shard_map/reduce_scatter | solution.py:204
  417.4 56.3 %all-gather.17.cloned.1.call-start = ((), (), s32[]{:S(2)}) async-start(), calls=%async_computation.27 | async-start | bytes 1658880 | tf_op jit(solution)/shard_map/all_gather | solution.py:195
  447.6 128.6 %reduce-scatter.33.cloned.1.call-start = ((), (), s32[]{:S(2)}) async-start(), calls=%async_computation.28 | async-start | bytes 921600 | tf_op jit(solution)/shard_map/reduce_scatter | solution.py:201
  501.3 78.4 %reduce-scatter.35.cloned.1.call-start = ((), (), s32[]{:S(2)}) async-start(), calls=%async_computation.29 | async-start | bytes 1658880 | tf_op jit(solution)/shard_map/reduce_scatter | solution.py:204
  515.8 542.5 %all-reduce.8.cloned.1.call-start = ((), (), s32[]{:S(2)}) async-start(), calls=%async_computation.31 | async-start | bytes 33030144 | tf_op jit(solution)/shard_map/psum | solution.py:375
  537.7 655.7 %all-reduce.6.cloned.1.call-start = ((), (), s32[]{:S(2)}) async-start(), calls=%async_computation.30 | async-start | bytes 221184 | tf_op jit(solution)/shard_map/psum | solution.py:384
  1063.7 136.4 %copy-start.1 = (bf16[5,768]{1,0:T(8,128)(2,1)S(1)}, bf16[5,768]{1,0:T(8,128)(2,1)}, u32[]{:S(2)}) copy-start(bf16[5,768]{1,0:T(8,128)(2,1)} %param.24) | copy-start | bytes 23044
  (163 other events, 783.5 us)
Sparse Core Ops, SparseCore 0:
  10.6 19.4 all-gather.6
  44.5 26.5 reduce-scatter.18
  73.6 22.9 reduce-scatter.12
  98.6 18.2 all-gather.8
  150.6 26.5 reduce-scatter.20
  179.5 22.9 reduce-scatter.14
  204.6 18.2 all-gather.10
  225.4 22.9 reduce-scatter.16
  251.0 26.4 reduce-scatter.22
  281.6 19.6 all-gather.12
  303.8 23.4 reduce-scatter.24
  329.7 26.4 reduce-scatter.28
  359.9 18.2 all-gather.14
  381.6 22.9 reduce-scatter.26
  417.5 26.5 reduce-scatter.30
  447.7 18.2 all-gather.16
  501.4 22.9 reduce-scatter.32
  526.8 26.4 reduce-scatter.34
  558.1 500.1 all-reduce.7
  1065.7 127.6 all-reduce.5
where the time goes:
time: 1220 us; the launch traced here: 1210 us
  waiting for transfers between devices  744 us (61%)
  matrix products  168 us (14%)
  local copies, waits for them, and re-layouts  135 us (11%)
  blocking collectives  86.1 us (7%)
  other arithmetic  56.2 us (5%)
  between operations  16.8 us (1%)
    psum x1, waiting for transfers between devices, body(): lax.psum((attn_in_grads, attn_out_grads, ffn_in_grads, ffn_out_grads, qv_...  475 us
    psum x1, waiting for transfers between devices, body(): lax.psum((task_part, group_part, offset_part, gain_part, shift_part), ('d...  125 us
    reduce_scatter x3, waiting for transfers between devices, scatter_rows(): lax.psum_scatter(former.astype(jnp.bfloat16), 'tensor', scatter_dimension...  62.8 us
    dot_general x24, matrix products, linear(): return jnp.dot(source, weight, preferred_element_type=jnp.float32)  47 us
    dot_general x20, matrix products, linear_back(): lax.dot_general(upstream, weight, (((1,), (1,)), ((), ())), preferred_ele...  44.5 us
    reshape x24, local copies, waits for them, and re-layouts, split_heads(): flattened.reshape(item_count, flattened.shape[0] // item_count, flattened...  42.9 us
    psum x1, blocking collectives, body(): lax.psum((attn_in_grads, attn_out_grads, ffn_in_grads, ffn_out_grads, qv_...  35.1 us
    unnamed x341, local copies, waits for them, and re-layouts  33.4 us
  transfers between devices with their start and end apart: 20, of which 13 were waited for; matrix products, arithmetic and copies ran while one was open for 20% of the time, Pallas kernels for 0%

commit v1 on v0

--- a/solution.py
+++ b/solution.py
@@ -1,6 +1,10 @@
+import functools
+
 import jax
 import jax.numpy as jnp
 from jax import lax
+from jax.experimental import pallas as pl
+from jax.experimental.pallas import tpu as pltpu
 from jax.sharding import PartitionSpec as P
 
 HEAD = 64
@@ -158,13 +162,11 @@
 
 def projection_grads(source_q, source_kv, weights, grad_set):
     grad_query, grad_keys, grad_values = grad_set
-    w_grads = jnp.stack(
-        [
-            weight_grad(source_q, grad_query),
-            weight_grad(source_kv, grad_keys),
-            weight_grad(source_kv, grad_values),
-        ]
-    )
+    w_grads = [
+        weight_grad(source_q, grad_query),
+        weight_grad(source_kv, grad_keys),
+        weight_grad(source_kv, grad_values),
+    ]
     b_grads = jnp.stack([column_sum(grad_query), column_sum(grad_values)])
     back_query = linear_back(grad_query, weights[0])
     back_kv = linear_back(grad_keys, weights[1]) + linear_back(grad_values, weights[2])
@@ -205,6 +207,85 @@
             latter.astype(jnp.bfloat16), "tensor", scatter_dimension=0, tiled=True
         ).astype(jnp.float32),
     )
+
+
+def flipped_grad(source, upstream):
+    return weight_grad(upstream, source)
+
+
+def share_sum(grads):
+    joined = jnp.concatenate([g.astype(jnp.bfloat16) for g in grads], axis=1)
+    return lax.psum_scatter(joined, "dp", scatter_dimension=0, tiled=True)
+
+
+def small_sum_kernel(n_dp, n_tensor, wide, x_ref, o_ref, held, landed, send_sem, recv_sem):
+    dp = lax.axis_index("dp")
+    tensor = lax.axis_index("tensor")
+    hops = []
+    bit = 1
+    while bit < n_tensor:
+        hops.append((False, bit))
+        bit *= 2
+    bit = 1
+    while bit < n_dp:
+        hops.append((True, bit))
+        bit *= 2
+
+    def flip(index, bit):
+        return index + bit - 2 * bit * lax.rem(index // bit, 2)
+
+    def partner(along_dp, bit):
+        return (flip(dp, bit), tensor) if along_dp else (dp, flip(tensor, bit))
+
+    barrier = pltpu.get_barrier_semaphore()
+    for hop in hops:
+        pl.semaphore_signal(
+            barrier, inc=1, device_id=partner(*hop), device_id_type=pl.DeviceIdType.MESH
+        )
+    pl.semaphore_wait(barrier, len(hops))
+    held[0] = x_ref[...]
+    for step, hop in enumerate(hops):
+        rows = x_ref.shape[0] if hop[0] else wide
+        copy = pltpu.make_async_remote_copy(
+            src_ref=held.at[step, pl.ds(0, rows)],
+            dst_ref=landed.at[step, pl.ds(0, rows)],
+            send_sem=send_sem.at[step],
+            recv_sem=recv_sem.at[step],
+            device_id=partner(*hop),
+            device_id_type=pl.DeviceIdType.MESH,
+        )
+        copy.start()
+        copy.wait()
+        if rows < x_ref.shape[0]:
+            held[step + 1, pl.ds(0, rows)] = (
+                held[step, pl.ds(0, rows)] + landed[step, pl.ds(0, rows)]
+            )
+            held[step + 1, pl.ds(rows, x_ref.shape[0] - rows)] = held[
+                step, pl.ds(rows, x_ref.shape[0] - rows)
+            ]
+        else:
+            held[step + 1] = held[step] + landed[step]
+    o_ref[...] = held[len(hops)]
+
+
+def small_sum(stacked, wide):
+    n_dp, n_tensor = lax.axis_size("dp"), lax.axis_size("tensor")
+    steps = n_dp.bit_length() + n_tensor.bit_length() - 2
+    vmem = pl.BlockSpec(memory_space=pltpu.VMEM)
+    return pl.pallas_call(
+        functools.partial(small_sum_kernel, n_dp, n_tensor, wide),
+        out_shape=jax.ShapeDtypeStruct(stacked.shape, jnp.float32),
+        in_specs=[vmem],
+        out_specs=vmem,
+        scratch_shapes=[
+            pltpu.VMEM((steps + 1,) + stacked.shape, jnp.float32),
+            pltpu.VMEM((steps,) + stacked.shape, jnp.float32),
+            pltpu.SemaphoreType.DMA((steps,)),
+            pltpu.SemaphoreType.DMA((steps,)),
+        ],
+        compiler_params=pltpu.CompilerParams(collective_id=0, has_side_effects=True),
+        name="small_sum",
+    )(stacked)
 
 
 def body(
@@ -255,10 +336,12 @@
     lang_low = lang_base.astype(jnp.bfloat16)
     visn_low = visn_base.astype(jnp.bfloat16)
     lang_all, visn_all = gather_rows(lang_low, visn_low)
-    cross_lang = attend_forward(lang_all, visn_all, None, attn_in[0], qv_bias[0], item_count)[0]
-    cross_visn = attend_forward(visn_all, lang_all, keep_words, attn_in[0], qv_bias[0], item_count)[
-        0
-    ]
+    cross_lang, saved_cross_lang = attend_forward(
+        lang_all, visn_all, None, attn_in[0], qv_bias[0], item_count
+    )
+    cross_visn, saved_cross_visn = attend_forward(
+        visn_all, lang_all, keep_words, attn_in[0], qv_bias[0], item_count
+    )
     part_lang, part_visn = scatter_rows(
         linear(cross_lang, attn_out[0]), linear(cross_visn, attn_out[0])
     )
@@ -293,10 +376,16 @@
     down_lang, down_visn = gather_grads(
         top_lang.astype(jnp.bfloat16), top_visn.astype(jnp.bfloat16)
     )
-    ffn_out_grads = jnp.stack([weight_grad(act_lang, down_lang), weight_grad(act_visn, down_visn)])
     inner_lang = (linear_back(down_lang, ffn_out[0]) * gelu_slope(pre_lang)).astype(jnp.bfloat16)
     inner_visn = (linear_back(down_visn, ffn_out[1]) * gelu_slope(pre_visn)).astype(jnp.bfloat16)
-    ffn_in_grads = jnp.stack([weight_grad(ffn_lang, inner_lang), weight_grad(ffn_visn, inner_visn)])
+    ffn_share = share_sum(
+        [
+            weight_grad(ffn_lang, inner_lang),
+            weight_grad(ffn_visn, inner_visn),
+            flipped_grad(act_lang, down_lang),
+            flipped_grad(act_visn, down_visn),
+        ]
+    )
     ffn_bias_grads = jnp.stack([column_sum(inner_lang), column_sum(inner_visn)])
     back_lang, back_visn = scatter_grads(
         linear_back(inner_lang, ffn_in[0]), linear_back(inner_visn, ffn_in[1])
@@ -306,8 +395,8 @@
     top_lang, gain_l1, shift_l1, offset_l1 = norm_backward(grad_two_lang, stash_l1, gains[1])
     top_visn, gain_v2, shift_v2, offset_v2 = norm_backward(grad_two_visn, stash_v2, gains[2])
     mid_lang, mid_visn = gather_grads(top_lang.astype(jnp.bfloat16), top_visn.astype(jnp.bfloat16))
-    out_grad_lang = weight_grad(ctx_lang, mid_lang)
-    out_grad_visn = weight_grad(ctx_visn, mid_visn)
+    out_grad_lang = flipped_grad(ctx_lang, mid_lang)
+    out_grad_visn = flipped_grad(ctx_visn, mid_visn)
     grads_lang = attend_backward(linear_back(mid_lang, attn_out[1]), saved_lang, item_count)
     grads_visn = attend_backward(linear_back(mid_visn, attn_out[2]), saved_visn, item_count)
     win_lang, bias_lang, query_lang, kv_lang = projection_grads(
@@ -316,6 +405,7 @@
     win_visn, bias_visn, query_visn, kv_visn = projection_grads(
         self_visn, self_visn, attn_in[2], grads_visn
     )
+    self_share = share_sum(win_lang + win_visn + [out_grad_lang, out_grad_visn])
     back_lang, back_visn = scatter_grads(query_lang + kv_lang, query_visn + kv_visn)
     grad_one_lang = top_lang + back_lang
     grad_one_visn = top_visn + back_visn
@@ -324,17 +414,7 @@
     cross_dlang, cross_dvisn = gather_grads(
         top_lang.astype(jnp.bfloat16), top_visn.astype(jnp.bfloat16)
     )
-    again_lang, again_visn = (
-        lax.all_gather(lang_low, "tensor", axis=0, tiled=True),
-        lax.all_gather(visn_low, "tensor", axis=0, tiled=True),
-    )
-    redo_lang, saved_cross_lang = attend_forward(
-        again_lang, again_visn, None, attn_in[0], qv_bias[0], item_count
-    )
-    redo_visn, saved_cross_visn = attend_forward(
-        again_visn, again_lang, keep_words, attn_in[0], qv_bias[0], item_count
-    )
-    cross_out_grad = weight_grad(redo_lang, cross_dlang) + weight_grad(redo_visn, cross_dvisn)
+    cross_out_grad = flipped_grad(cross_lang, cross_dlang) + flipped_grad(cross_visn, cross_dvisn)
     grads_cross_lang = attend_backward(
         linear_back(cross_dlang, attn_out[0]), saved_cross_lang, item_count
     )
@@ -342,19 +422,20 @@
         linear_back(cross_dvisn, attn_out[0]), saved_cross_visn, item_count
     )
     win_first, bias_first, query_from_lang, kv_from_visn = projection_grads(
-        again_lang, again_visn, attn_in[0], grads_cross_lang
+        lang_all, visn_all, attn_in[0], grads_cross_lang
     )
     win_second, bias_second, query_from_visn, kv_from_lang = projection_grads(
-        again_visn, again_lang, attn_in[0], grads_cross_visn
+        visn_all, lang_all, attn_in[0], grads_cross_visn
+    )
+    cross_share = share_sum(
+        [first + second for first, second in zip(win_first, win_second)] + [cross_out_grad]
     )
     back_lang, back_visn = scatter_grads(
         query_from_lang + kv_from_lang, query_from_visn + kv_from_visn
     )
     base_grad_lang = top_lang + back_lang
     base_grad_visn = top_visn + back_visn
-    attn_in_grads = jnp.stack([win_first + win_second, win_lang, win_visn])
     qv_grads = jnp.stack([bias_first + bias_second, bias_lang, bias_visn])
-    attn_out_grads = jnp.stack([cross_out_grad, out_grad_lang, out_grad_visn])
     offset_part = jnp.stack([offset_l0 + offset_v0, offset_l1, offset_v2, offset_l3, offset_v4])
     gain_part = jnp.stack([gain_l0 + gain_v0, gain_l1, gain_v2, gain_l3, gain_v4])
     shift_part = jnp.stack([shift_l0 + shift_v0, shift_l1, shift_v2, shift_l3, shift_v4])
@@ -372,18 +453,34 @@
         precision=highest,
         preferred_element_type=jnp.float32,
     )
-    attn_in_sum, attn_out_sum, ffn_in_sum, ffn_out_sum, qv_grads, ffn_bias_grads = lax.psum(
-        (attn_in_grads, attn_out_grads, ffn_in_grads, ffn_out_grads, qv_grads, ffn_bias_grads), "dp"
-    )
-    share_rows = attn_in_sum.shape[2] // lax.axis_size("dp")
-    share_start = lax.axis_index("dp") * share_rows
-    attn_in_grads = lax.dynamic_slice_in_dim(attn_in_sum, share_start, share_rows, 2)
-    attn_out_grads = lax.dynamic_slice_in_dim(attn_out_sum, share_start, share_rows, 2)
-    ffn_in_grads = lax.dynamic_slice_in_dim(ffn_in_sum, share_start, share_rows, 1)
-    ffn_out_grads = lax.dynamic_slice_in_dim(ffn_out_sum, share_start, share_rows, 2)
-    task_grad, group_grad, offset_grad, gain_grad, shift_grad = lax.psum(
-        (task_part, group_part, offset_part, gain_part, shift_part), ("dp", "tensor")
-    )
+    head_cols = attn_in.shape[3]
+    hidden_cols = ffn_in.shape[2]
+    share_rows = cross_share.shape[0]
+    cross_parts = cross_share.astype(jnp.float32).reshape(share_rows, 4, head_cols)
+    self_parts = self_share.astype(jnp.float32).reshape(share_rows, 8, head_cols)
+    ffn_parts = ffn_share.astype(jnp.float32).reshape(share_rows, 4, hidden_cols)
+    attn_in_grads = jnp.stack(
+        [
+            cross_parts[:, 0:3].transpose(1, 0, 2),
+            self_parts[:, 0:3].transpose(1, 0, 2),
+            self_parts[:, 3:6].transpose(1, 0, 2),
+        ]
+    )
+    attn_out_grads = jnp.stack([cross_parts[:, 3].T, self_parts[:, 6].T, self_parts[:, 7].T])
+    ffn_in_grads = ffn_parts[:, 0:2].transpose(1, 0, 2)
+    ffn_out_grads = ffn_parts[:, 2:4].transpose(1, 2, 0)
+    width = task_part.shape[1]
+    wide_rows = jnp.concatenate(
+        [task_part, group_part, offset_part, gain_part, shift_part, jnp.zeros((1, width))]
+    )
+    bias_rows = jnp.concatenate(
+        [ffn_bias_grads, jnp.pad(qv_grads.reshape(6, head_cols), ((0, 0), (0, width - head_cols)))]
+    )
+    summed = small_sum(jnp.concatenate([wide_rows, bias_rows]), wide_rows.shape[0])
+    task_grad, group_grad = summed[0:3], summed[3:8]
+    offset_grad, gain_grad, shift_grad = summed[8:13], summed[13:18], summed[18:23]
+    ffn_bias_grads = summed[24:26]
+    qv_grads = summed[26:32, :head_cols].reshape(3, 2, head_cols)
     return (
         lang_out.astype(jnp.bfloat16),
         visn_out.astype(jnp.bfloat16),

time: 1220 us -> 830 us (0.68)
  waiting for transfers between devices: 744 us -> 386 us
  blocking collectives: 86.1 us -> 49.7 us
  Pallas kernels: 0 us -> 19.8 us
  other arithmetic: 56.2 us -> 40.4 us
    psum x2 -> x0, waiting for transfers between devices: 600 us -> none  [the longest x1 475 us: body(): lax.psum((attn_in_grads, attn_out_grads, ffn_in_grads, ffn_out_grads, qv_...]
    unnamed x20 -> x24, waiting for transfers between devices: 0.33 us -> 162 us
    psum x1 -> x0, blocking collectives: 35.1 us -> none  [body(): lax.psum((attn_in_grads, attn_out_grads, ffn_in_grads, ffn_out_grads, qv_...]
    reduce_scatter x3, waiting for transfers between devices: 10.7 us -> 41 us  [scatter_grads(): lax.psum_scatter(former.astype(jnp.bfloat16), 'tensor', scatter_dimension...]
    reduce_scatter x3, waiting for transfers between devices: 12.1 us -> 37.5 us  [scatter_grads(): lax.psum_scatter(latter.astype(jnp.bfloat16), 'tensor', scatter_dimension...]
    all_gather x3, waiting for transfers between devices: 0.04 us -> 23.1 us  [gather_grads(): lax.all_gather(latter, 'tensor', axis=0, tiled=True)]
    pallas_call x0 -> x1, Pallas kernels: none -> 19.8 us  [small_sum(): pl.pallas_call(functools.partial(small_sum_kernel, n_dp, n_tensor, wide),...]
    another operation x7 -> x2, other arithmetic: 15.6 us -> 0.81 us  [the longest x1 0.75 us: body(): jnp.stack([cross_parts[:, 3].T, self_parts[:, 6].T, self_parts[:, 7].T])]
  transfers between devices with their start and end apart: 20 -> 21, of which waited for: 13 -> 15; matrix products, arithmetic and copies ran while one was open for 20% -> 28% of each run, Pallas kernels for 0% -> 0%
where the time goes in v1:
time: 830 us; the launch traced here: 817 us
  waiting for transfers between devices  386 us (47%)
  matrix products  166 us (20%)
  local copies, waits for them, and re-layouts  136 us (16%)
  blocking collectives  49.7 us (6%)
  other arithmetic  40.4 us (5%)
  Pallas kernels  19.8 us (2%)
  between operations  16.8 us (2%)
    unnamed x24, waiting for transfers between devices  162 us
    reduce_scatter x3, waiting for transfers between devices, scatter_rows(): lax.psum_scatter(former.astype(jnp.bfloat16), 'tensor', scatter_dimension...  56.2 us
    dot_general x24, matrix products, linear(): return jnp.dot(source, weight, preferred_element_type=jnp.float32)  48.5 us
    reshape x24, local copies, waits for them, and re-layouts, split_heads(): flattened.reshape(item_count, flattened.shape[0] // item_count, flattened...  43.3 us
    dot_general x20, matrix products, linear_back(): lax.dot_general(upstream, weight, (((1,), (1,)), ((), ())), preferred_ele...  42.4 us
    all_gather x3, waiting for transfers between devices, gather_rows(): lax.all_gather(latter, 'tensor', axis=0, tiled=True)  41.2 us
    reduce_scatter x3, waiting for transfers between devices, scatter_grads(): lax.psum_scatter(former.astype(jnp.bfloat16), 'tensor', scatter_dimension...  41 us
    unnamed x349, local copies, waits for them, and re-layouts  40 us
  transfers between devices with their start and end apart: 21, of which 15 were waited for; matrix products, arithmetic and copies ran while one was open for 28% of the time, Pallas kernels for 0%

profile of v1, /device:TPU:8, one launch (start us, length us, event | category | flops | bytes accessed | tf_op | source)
XLA Modules:
  0.0 817.0 jit_solution(12630324657362317648)
XLA Ops:
  11.6 8.4 %all_gather.37 = bf16[480,768]{1,0:T(8,128)(2,1)S(1)} all-gather(bf16[120,768]{1,0:T(8,128)(2,1)S(1)} %get-tuple-element.149), channel_id=1, replica_groups=mesh['dp'=8,'tensor'=4] {'tensor'}, dimensions={0}, use_global_device_ids=true | all-gather | bytes 921600 | tf_op jit(solution)/shard_map/all_gather | solution.py:178
  47.8 25.3 %reduce-scatter.28.cloned.1.call-done = bf16[216,768]{1,0:T(8,128)(2,1)} async-done(((bf16[864,768]{1,0:T(8,128)(2,1)}), bf16[216,768]{1,0:T(8,128)(2,1)}) %reduce-scatter.28.cloned.1.call-update) | async-done | bytes 331792 | tf_op jit(solution)/shard_map/reduce_scatter | solution.py:188
  76.0 17.8 %all-gather.9.cloned.1.call-done = bf16[864,768]{1,0:T(8,128)(2,1)} async-done(((bf16[216,768]{1,0:T(8,128)(2,1)}), bf16[864,768]{1,0:T(8,128)(2,1)}) %all-gather.9.cloned.1.call-update) | async-done | bytes 1327120 | tf_op jit(solution)/shard_map/all_gather | solution.py:179
  152.9 20.2 %reduce-scatter.22.cloned.1.call-done = bf16[120,768]{1,0:T(8,128)(2,1)} async-done(((bf16[480,768]{1,0:T(8,128)(2,1)}), bf16[120,768]{1,0:T(8,128)(2,1)}) %reduce-scatter.22.cloned.1.call-update) | async-done | bytes 184336 | tf_op jit(solution)/shard_map/reduce_scatter | solution.py:185
  174.2 19.2 %all-gather.11.cloned.1.call-done = bf16[864,768]{1,0:T(8,128)(2,1)} async-done(((bf16[216,768]{1,0:T(8,128)(2,1)}), bf16[864,768]{1,0:T(8,128)(2,1)}) %all-gather.11.cloned.1.call-update) | async-done | bytes 1327120 | tf_op jit(solution)/shard_map/all_gather | solution.py:179
  201.8 8.5 %all_gather.38 = bf16[480,768]{1,0:T(8,128)(2,1)S(1)} all-gather(bf16[120,768]{1,0:T(8,128)(2,1)S(1)} %fusion.122), channel_id=1, replica_groups=mesh['dp'=8,'tensor'=4] {'tensor'}, dimensions={0}, use_global_device_ids=true | all-gather | bytes 921600 | tf_op jit(solution)/shard_map/all_gather | solution.py:178
  242.9 19.1 %reduce-scatter.24.cloned.1.call-done = bf16[120,768]{1,0:T(8,128)(2,1)} async-done(((bf16[480,768]{1,0:T(8,128)(2,1)}), bf16[120,768]{1,0:T(8,128)(2,1)}) %reduce-scatter.24.cloned.1.call-update) | async-done | bytes 184336 | tf_op jit(solution)/shard_map/reduce_scatter | solution.py:185
  263.7 7.8 all_gather.39
  276.1 6.3 all-gather.13.cloned.1.call-done
  282.4 5.0 convert_reduce_fusion
  290.9 16.9 %reduce-scatter.26.cloned.1.call-done = bf16[120,768]{1,0:T(8,128)(2,1)} async-done(((bf16[480,768]{1,0:T(8,128)(2,1)}), bf16[120,768]{1,0:T(8,128)(2,1)}) %reduce-scatter.26.cloned.1.call-update) | async-done | bytes 184336 | tf_op jit(solution)/shard_map/reduce_scatter | solution.py:185
  312.2 8.1 all_gather.42
  324.6 12.4 %reduce-scatter.38.cloned.1.call-done = bf16[216,768]{1,0:T(8,128)(2,1)} async-done(((bf16[864,768]{1,0:T(8,128)(2,1)}), bf16[216,768]{1,0:T(8,128)(2,1)}) %reduce-scatter.38.cloned.1.call-update) | async-done | bytes 331792 | tf_op jit(solution)/shard_map/reduce_scatter | solution.py:206
  340.6 21.8 %reduce-scatter.34.cloned.1.call-done = bf16[120,768]{1,0:T(8,128)(2,1)} async-done(((bf16[480,768]{1,0:T(8,128)(2,1)}), bf16[120,768]{1,0:T(8,128)(2,1)}) %reduce-scatter.34.cloned.1.call-update) | async-done | bytes 184336 | tf_op jit(solution)/shard_map/reduce_scatter | solution.py:203
  366.0 16.7 %all-gather.15.cloned.1.call-done = bf16[864,768]{1,0:T(8,128)(2,1)} async-done(((bf16[216,768]{1,0:T(8,128)(2,1)}), bf16[864,768]{1,0:T(8,128)(2,1)}) %all-gather.15.cloned.1.call-update) | async-done | bytes 1327120 | tf_op jit(solution)/shard_map/all_gather | solution.py:197
  412.1 8.5 %all_gather.43 = bf16[480,768]{1,0:T(8,128)(2,1)S(1)} all-gather(bf16[120,768]{1,0:T(8,128)(2,1)S(1)} %copy-done.74), channel_id=1, replica_groups=mesh['dp'=8,'tensor'=4] {'tensor'}, dimensions={0}, use_global_device_ids=true | all-gather | bytes 921600 | tf_op jit(solution)/shard_map/all_gather | solution.py:196
  475.3 6.7 copy.222
  485.3 8.4 %all_gather.44 = bf16[480,768]{1,0:T(8,128)(2,1)S(1)} all-gather(bf16[120,768]{1,0:T(8,128)(2,1)S(1)} %convert_element_type.594), channel_id=1, replica_groups=mesh['dp'=8,'tensor'=4] {'tensor'}, dimensions={0}, use_global_device_ids=true | all-gather | bytes 921600 | tf_op jit(solution)/shard_map/all_gather | solution.py:196
  506.1 6.5 convert_reduce_fusion.4
  562.3 96.6 %reduce-scatter.50.cloned.1.call-done = bf16[96,3072]{1,0:T(8,128)(2,1)} async-done(((bf16[768,3072]{1,0:T(8,128)(2,1)}), bf16[96,3072]{1,0:T(8,128)(2,1)}) %reduce-scatter.50.cloned.1.call-update) | async-done | bytes 589840
  664.5 19.3 %reduce-scatter.42.cloned.1.call-done = bf16[120,768]{1,0:T(8,128)(2,1)} async-done(((bf16[480,768]{1,0:T(8,128)(2,1)}), bf16[120,768]{1,0:T(8,128)(2,1)}) %reduce-scatter.42.cloned.1.call-update) | async-done | bytes 184336 | tf_op jit(solution)/shard_map/reduce_scatter | solution.py:203
  686.7 64.7 %reduce-scatter.46.cloned.1.call-done = bf16[96,768]{1,0:T(8,128)(2,1)} async-done(((bf16[768,768]{1,0:T(8,128)(2,1)}), bf16[96,768]{1,0:T(8,128)(2,1)}) %reduce-scatter.46.cloned.1.call-update) | async-done | bytes 147472
  754.7 25.1 %reduce-scatter.44.cloned.1.call-done = bf16[216,768]{1,0:T(8,128)(2,1)} async-done(((bf16[864,768]{1,0:T(8,128)(2,1)}), bf16[216,768]{1,0:T(8,128)(2,1)}) %reduce-scatter.44.cloned.1.call-update) | async-done | bytes 331792 | tf_op jit(solution)/shard_map/reduce_scatter | solution.py:206
  783.9 19.8 %small_sum.1 = f32[32,768]{1,0:T(8,128)} custom-call(f32[32,768]{1,0:T(8,128)} %concatenate.26.x_ref), custom_call_target="tpu_custom_call" | custom-call | tf_op jit(solution)/shard_map/small_sum/pallas_call | solution.py:275
  (675 shorter events, 331.1 us)
Async XLA Ops:
  7.2 22.6 %all-gather.7.cloned.1.call-start = ((), (), s32[]{:S(2)}) async-start(), calls=%async_computation.15 | async-start | bytes 1658880 | tf_op jit(solution)/shard_map/all_gather | solution.py:179
  10.3 62.8 %reduce-scatter.28.cloned.1.call-start = ((), (), s32[]{:S(2)}) async-start(), calls=%async_computation.19 | async-start | bytes 1658880 | tf_op jit(solution)/shard_map/reduce_scatter | solution.py:188
  20.0 101.3 %copy-start.3 = (bf16[480,768]{1,0:T(8,128)(2,1)}, bf16[480,768]{1,0:T(8,128)(2,1)S(1)}, u32[]{:S(2)}) copy-start(bf16[480,768]{1,0:T(8,128)(2,1)S(1)} %all_gather.37) | copy-start | bytes 2211844
  46.4 47.4 %all-gather.9.cloned.1.call-start = ((), (), s32[]{:S(2)}) async-start(), calls=%async_computation.20 | async-start | bytes 1658880 | tf_op jit(solution)/shard_map/all_gather | solution.py:179
  75.4 74.1 %reduce-scatter.30.cloned.1.call-start = ((), (), s32[]{:S(2)}) async-start(), calls=%async_computation.21 | async-start | bytes 1658880 | tf_op jit(solution)/shard_map/reduce_scatter | solution.py:188
  121.1 52.0 %reduce-scatter.22.cloned.1.call-start = ((), (), s32[]{:S(2)}) async-start(), calls=%async_computation.16 | async-start | bytes 921600 | tf_op jit(solution)/shard_map/reduce_scatter | solution.py:185
  149.5 43.9 %all-gather.11.cloned.1.call-start = ((), (), s32[]{:S(2)}) async-start(), calls=%async_computation.22 | async-start | bytes 1658880 | tf_op jit(solution)/shard_map/all_gather | solution.py:179
  151.2 46.8 %copy-start.99 = (f32[216]{0:T(256)}, f32[216]{0:T(256)S(1)}, u32[]{:S(2)}) copy-start(f32[216]{0:T(256)S(1)} %add_rsqrt_fusion.1) | copy-start | bytes 2596
  152.2 86.7 %reduce-scatter.32.cloned.1.call-start = ((), (), s32[]{:S(2)}) async-start(), calls=%async_computation.23 | async-start | bytes 1658880 | tf_op jit(solution)/shard_map/reduce_scatter | solution.py:188
  201.4 60.6 %reduce-scatter.24.cloned.1.call-start = ((), (), s32[]{:S(2)}) async-start(), calls=%async_computation.17 | async-start | bytes 921600 | tf_op jit(solution)/shard_map/reduce_scatter | solution.py:185
  238.8 43.6 %all-gather.13.cloned.1.call-start = ((), (), s32[]{:S(2)}) async-start(), calls=%async_computation.26 | async-start | bytes 1658880 | tf_op jit(solution)/shard_map/all_gather | solution.py:197
  242.9 64.9 %reduce-scatter.26.cloned.1.call-start = ((), (), s32[]{:S(2)}) async-start(), calls=%async_computation.18 | async-start | bytes 921600 | tf_op jit(solution)/shard_map/reduce_scatter | solution.py:185
  276.1 60.9 %reduce-scatter.38.cloned.1.call-start = ((), (), s32[]{:S(2)}) async-start(), calls=%async_computation.27 | async-start | bytes 1658880 | tf_op jit(solution)/shard_map/reduce_scatter | solution.py:206
  290.9 71.5 %reduce-scatter.34.cloned.1.call-start = ((), (), s32[]{:S(2)}) async-start(), calls=%async_computation.24 | async-start | bytes 921600 | tf_op jit(solution)/shard_map/reduce_scatter | solution.py:203
  324.6 58.2 %all-gather.15.cloned.1.call-start = ((), (), s32[]{:S(2)}) async-start(), calls=%async_computation.28 | async-start | bytes 1658880 | tf_op jit(solution)/shard_map/all_gather | solution.py:197
  340.5 102.7 %reduce-scatter.40.cloned.1.call-start = ((), (), s32[]{:S(2)}) async-start(), calls=%async_computation.29 | async-start | bytes 1658880 | tf_op jit(solution)/shard_map/reduce_scatter | solution.py:206
  412.0 70.0 %reduce-scatter.36.cloned.1.call-start = ((), (), s32[]{:S(2)}) async-start(), calls=%async_computation.25 | async-start | bytes 921600 | tf_op jit(solution)/shard_map/reduce_scatter | solution.py:203
  443.2 79.3 %all-gather.17.cloned.1.call-start = ((), (), s32[]{:S(2)}) async-start(), calls=%async_computation.30 | async-start | bytes 1658880 | tf_op jit(solution)/shard_map/all_gather | solution.py:197
  447.3 113.0 %reduce-scatter.48.cloned.1.call-start = ((), (), s32[]{:S(2)}) async-start(), calls=%async_computation.34 | async-start | bytes 2654208
  464.6 194.2 %reduce-scatter.50.cloned.1.call-start = ((), (), s32[]{:S(2)}) async-start(), calls=%async_computation.35 | async-start | bytes 5308416
  482.0 201.8 %reduce-scatter.42.cloned.1.call-start = ((), (), s32[]{:S(2)}) async-start(), calls=%async_computation.31 | async-start | bytes 921600 | tf_op jit(solution)/shard_map/reduce_scatter | solution.py:203
  545.7 205.7 %reduce-scatter.46.cloned.1.call-start = ((), (), s32[]{:S(2)}) async-start(), calls=%async_computation.33 | async-start | bytes 1327104
  553.2 226.6 %reduce-scatter.44.cloned.1.call-start = ((), (), s32[]{:S(2)}) async-start(), calls=%async_computation.32 | async-start | bytes 1658880 | tf_op jit(solution)/shard_map/reduce_scatter | solution.py:206
  753.9 56.0 %copy-start.1 = (bf16[5,768]{1,0:T(8,128)(2,1)S(1)}, bf16[5,768]{1,0:T(8,128)(2,1)}, u32[]{:S(2)}) copy-start(bf16[5,768]{1,0:T(8,128)(2,1)} %param.24) | copy-start | bytes 23044
  (167 other events, 877.9 us)
Sparse Core Ops, SparseCore 0:
  10.4 19.4 all-gather.6
  46.5 26.5 reduce-scatter.27
  75.5 18.2 all-gather.8
  121.2 26.5 reduce-scatter.29
  150.1 22.9 reduce-scatter.21
  175.1 18.2 all-gather.10
  201.5 26.4 reduce-scatter.31
  239.0 22.9 reduce-scatter.23
  264.1 18.2 all-gather.12
  284.8 22.9 reduce-scatter.25
  310.4 26.5 reduce-scatter.37
  339.4 22.9 reduce-scatter.33
  364.5 18.2 all-gather.14
  412.2 26.5 reduce-scatter.39
  443.3 22.9 reduce-scatter.35
  468.3 18.2 all-gather.16
  489.9 69.2 reduce-scatter.47
  562.7 96.0 reduce-scatter.49
  661.3 22.4 reduce-scatter.41
  687.0 64.3 reduce-scatter.45
  753.9 25.8 reduce-scatter.43
